TPU v7x, 128 devices: a whole 4x4x4 slice. The times are simulated.
128 devices in a mesh: pp: 2 (over core), dp: 64 (over z, y, x).
Axes of the slice: x: 4, y: 4, z: 4, core: 2. Of those that a mesh axis runs over, the one named last changes fastest.
Arguments:
- act_in: bfloat16 [8, 64, 384, 512], P(None, 'dp')
- loss_seed: bfloat16 [8, 64, 384, 512], P(None, 'dp')
- w_qkv: bfloat16 [2, 512, 24, 64], P('pp', 'dp')
- w_proj: bfloat16 [2, 512, 512], P('pp', 'dp')
- w_up: bfloat16 [2, 512, 2048], P('pp', 'dp')
- w_down: bfloat16 [2, 2048, 512], P('pp', 'dp')
Outputs:
- output 1: float32 [2, 512, 24, 64], P('pp', 'dp')
- output 2: float32 [2, 512, 512], P('pp', 'dp')
- output 3: float32 [2, 512, 2048], P('pp', 'dp')
- output 4: float32 [2, 2048, 512], P('pp', 'dp')
- output 5: bfloat16 [8, 64, 384, 512], P(None, 'dp', 'pp')
All inputs are finite; a program needn't handle non-finite values.
Results may differ from a plain program's by a relative error of at most 0.02.
Values are sent between devices in bfloat16 or wider.
A program may use at most 1 GiB of HBM per device.

v0:
```python
import jax
import jax.numpy as jnp
from jax import lax
from jax.sharding import PartitionSpec as P

NORM_EPS = 1e-6


def rms_norm(hidden):
    return hidden * lax.rsqrt(jnp.mean(hidden * hidden, axis=-1, keepdims=True) + NORM_EPS)


def gelu_tanh(pre_act):
    return jax.nn.gelu(pre_act, approximate=True)


def attn_core(q_heads, k_heads, v_heads):
    seq_len = q_heads.shape[1]
    scores = jnp.einsum('bqnh,bknh->bnqk', q_heads, k_heads, preferred_element_type=jnp.float32) * (q_heads.shape[-1] ** -0.5)
    causal = jnp.arange(seq_len)[:, None] >= jnp.arange(seq_len)[None, :]
    prob_bf = jax.nn.softmax(jnp.where(causal, scores, -1e30), axis=-1).astype(jnp.bfloat16)
    return jnp.einsum('bnqk,bknh->bqnh', prob_bf, v_heads, preferred_element_type=jnp.float32).astype(jnp.bfloat16)


def layer_forward(hidden, w_qkv, w_proj, w_up, w_down):
    num_heads = w_qkv.shape[1] // 3
    hid_f32 = hidden.astype(jnp.float32)
    normed = rms_norm(hid_f32).astype(jnp.bfloat16)
    qkv_act = jnp.einsum('bsd,dnh->bsnh', normed, w_qkv, preferred_element_type=jnp.float32).astype(jnp.bfloat16)
    q_heads = qkv_act[:, :, :num_heads]
    k_heads = qkv_act[:, :, num_heads:2 * num_heads]
    v_heads = qkv_act[:, :, 2 * num_heads:]
    attn_flat = attn_core(q_heads, k_heads, v_heads).reshape(hidden.shape)
    mid_f32 = (hid_f32 + jnp.einsum('bse,ed->bsd', attn_flat, w_proj, preferred_element_type=jnp.float32)).astype(jnp.bfloat16).astype(jnp.float32)
    normed2 = rms_norm(mid_f32).astype(jnp.bfloat16)
    up_act = jnp.einsum('bsd,df->bsf', normed2, w_up, preferred_element_type=jnp.float32).astype(jnp.bfloat16)
    gelu_out = gelu_tanh(up_act.astype(jnp.float32)).astype(jnp.bfloat16)
    block_out = (mid_f32 + jnp.einsum('bsf,fd->bsd', gelu_out, w_down, preferred_element_type=jnp.float32)).astype(jnp.bfloat16)
    saved_acts = (hid_f32, normed, q_heads, k_heads, v_heads, attn_flat, mid_f32, normed2, up_act, gelu_out)
    return block_out, saved_acts


def layer_backward(saved_acts, ct_out, w_qkv, w_proj, w_up, w_down):
    hid_f32, normed, q_heads, k_heads, v_heads, attn_flat, mid_f32, normed2, up_act, gelu_out = saved_acts
    g_down = jnp.einsum('bsf,bsd->fd', gelu_out, ct_out, preferred_element_type=jnp.float32)
    ct_gelu = jnp.einsum('bsd,fd->bsf', ct_out, w_down, preferred_element_type=jnp.float32).astype(jnp.bfloat16)
    gelu_pull = jax.vjp(gelu_tanh, up_act.astype(jnp.float32))[1]
    ct_up = gelu_pull(ct_gelu.astype(jnp.float32))[0].astype(jnp.bfloat16)
    g_up = jnp.einsum('bsd,bsf->df', normed2, ct_up, preferred_element_type=jnp.float32)
    ct_norm2 = jnp.einsum('bsf,df->bsd', ct_up, w_up, preferred_element_type=jnp.float32).astype(jnp.bfloat16)
    norm_pull2 = jax.vjp(rms_norm, mid_f32)[1]
    ct_mid = (ct_out.astype(jnp.float32) + norm_pull2(ct_norm2.astype(jnp.float32))[0]).astype(jnp.bfloat16)
    g_proj = jnp.einsum('bse,bsd->ed', attn_flat, ct_mid, preferred_element_type=jnp.float32)
    ct_attn = jnp.einsum('bsd,ed->bse', ct_mid, w_proj, preferred_element_type=jnp.float32).astype(jnp.bfloat16)
    attn_pull = jax.vjp(attn_core, q_heads, k_heads, v_heads)[1]
    ct_q, ct_k, ct_v = attn_pull(ct_attn.reshape(q_heads.shape))
    ct_qkv = jnp.concatenate([ct_q, ct_k, ct_v], axis=2)
    g_qkv = jnp.einsum('bsd,bsnh->dnh', normed, ct_qkv, preferred_element_type=jnp.float32)
    ct_norm = jnp.einsum('bsnh,dnh->bsd', ct_qkv, w_qkv, preferred_element_type=jnp.float32).astype(jnp.bfloat16)
    norm_pull = jax.vjp(rms_norm, hid_f32)[1]
    ct_hidden = (ct_mid.astype(jnp.float32) + norm_pull(ct_norm.astype(jnp.float32))[0]).astype(jnp.bfloat16)
    return ct_hidden, (g_qkv, g_proj, g_up, g_down)


def stage_forward(hidden, weights):
    for layer_idx in range(weights[0].shape[0]):
        hidden = layer_forward(hidden, weights[0][layer_idx], weights[1][layer_idx], weights[2][layer_idx], weights[3][layer_idx])[0]
    return hidden


def stage_backward(hidden, ct_out, weights):
    num_layers = weights[0].shape[0]
    saved_list = []
    for layer_idx in range(num_layers):
        layer_w = tuple(w_full[layer_idx] for w_full in weights)
        hidden, saved_acts = layer_forward(hidden, *layer_w)
        saved_list.append(saved_acts)
    grad_lists = ([], [], [], [])
    for layer_idx in reversed(range(num_layers)):
        layer_w = tuple(w_full[layer_idx] for w_full in weights)
        ct_out, layer_grads = layer_backward(saved_list[layer_idx], ct_out, *layer_w)
        for grad_list, grad_part in zip(grad_lists, layer_grads):
            grad_list.append(grad_part)
    return ct_out, tuple(jnp.stack(grad_list[::-1]) for grad_list in grad_lists)


def solution(mesh):
    stages = mesh.shape['pp']
    fwd_pairs = [(src_idx, src_idx + 1) for src_idx in range(stages - 1)]
    bwd_pairs = [(src_idx + 1, src_idx) for src_idx in range(stages - 1)]

    def device_step(act_in, loss_seed, w_qkv, w_proj, w_up, w_down):
        num_micro = act_in.shape[0]
        num_ticks = num_micro + 2 * stages - 2
        stage_idx = lax.axis_index('pp')
        weights = tuple(lax.all_gather(w_part, 'dp', axis=1, tiled=True) for w_part in (w_qkv, w_proj, w_up, w_down))
        zero_act = jnp.zeros(act_in.shape[1:], jnp.bfloat16)
        grad_init = tuple(jnp.zeros(w_full.shape, jnp.float32) for w_full in weights)

        def run_forward(hidden):
            return stage_forward(hidden, weights)

        def run_backward(hidden, ct_out, grad_acc):
            ct_in, stage_grads = stage_backward(hidden, ct_out, weights)
            return ct_in, tuple(acc_part + grad_part for acc_part, grad_part in zip(grad_acc, stage_grads))

        def skip_backward(hidden, ct_out, grad_acc):
            return jnp.zeros_like(hidden), grad_acc

        def run_tick(tick_idx, loop_state):
            fwd_buf, bwd_buf, stash_in, outputs, grad_acc = loop_state
            fwd_idx = tick_idx - stage_idx
            fwd_ok = (fwd_idx >= 0) & (fwd_idx < num_micro)
            fwd_slot = jnp.clip(fwd_idx, 0, num_micro - 1)
            fresh_in = lax.dynamic_index_in_dim(act_in, fwd_slot, 0, keepdims=False)
            stage_in = jnp.where(stage_idx == 0, fresh_in, fwd_buf)
            stage_out = lax.cond(fwd_ok, run_forward, jnp.zeros_like, stage_in)
            old_in = lax.dynamic_index_in_dim(stash_in, fwd_slot, 0, keepdims=False)
            stash_in = lax.dynamic_update_index_in_dim(stash_in, jnp.where(fwd_ok, stage_in, old_in), fwd_slot, 0)
            old_out = lax.dynamic_index_in_dim(outputs, fwd_slot, 0, keepdims=False)
            outputs = lax.dynamic_update_index_in_dim(outputs, jnp.where(fwd_ok, stage_out, old_out), fwd_slot, 0)
            bwd_idx = tick_idx - (2 * stages - 2) + stage_idx
            bwd_ok = (bwd_idx >= 0) & (bwd_idx < num_micro)
            bwd_slot = jnp.clip(bwd_idx, 0, num_micro - 1)
            seed_now = lax.dynamic_index_in_dim(loss_seed, bwd_slot, 0, keepdims=False)
            ct_out = jnp.where(stage_idx == stages - 1, seed_now, bwd_buf)
            saved_in = lax.dynamic_index_in_dim(stash_in, bwd_slot, 0, keepdims=False)
            ct_in, grad_acc = lax.cond(bwd_ok, run_backward, skip_backward, saved_in, ct_out, grad_acc)
            fwd_buf = lax.ppermute(stage_out, 'pp', fwd_pairs)
            bwd_buf = lax.ppermute(ct_in, 'pp', bwd_pairs)
            return fwd_buf, bwd_buf, stash_in, outputs, grad_acc

        loop_init = (zero_act, zero_act, jnp.zeros_like(act_in), jnp.zeros_like(act_in), grad_init)
        loop_state = lax.fori_loop(0, num_ticks, run_tick, loop_init)
        outputs, grad_acc = loop_state[3], loop_state[4]
        grad_shards = tuple(lax.psum_scatter(acc_part, 'dp', scatter_dimension=1, tiled=True) for acc_part in grad_acc)
        last_out = jnp.where(stage_idx == stages - 1, outputs, jnp.zeros_like(outputs))
        out_shard = lax.psum_scatter(last_out, 'pp', scatter_dimension=2, tiled=True)
        return grad_shards + (out_shard,)

    weight_spec = P('pp', 'dp')
    act_spec = P(None, 'dp')
    return jax.shard_map(device_step, mesh=mesh, in_specs=(act_spec, act_spec, weight_spec, weight_spec, weight_spec, weight_spec), out_specs=(weight_spec, weight_spec, weight_spec, weight_spec, P(None, 'dp', 'pp')), check_vma=False)
```

profile of v0, /device:TPU:0, one launch (start us, length us, event | category | flops | bytes accessed | tf_op | source)
XLA Modules:
  0.0 2278.3 jit_solution(14153080652558014892)
XLA Ops:
  9.4 181.2 %all_gather.13 = bf16[1,512,512]{2,1,0:T(8,128)(2,1)} all-gather(bf16[1,8,512]{2,1,0:T(8,128)(2,1)} %param.15), channel_id=1, replica_groups=mesh['pp'=2,'dp'=64] {'dp'}, dimensions={1}, use_global_device_ids=true | all-gather | bytes 532480 | tf_op jit(solution)/shard_map/all_gather | solution.py:96
  195.3 16.8 all-gather.8.cloned.1.call-done
  225.1 729.6 %while.29 = (s32[]{:T(128)}, bf16[1,384,512]{2,1,0:T(8,128)(2,1)}, bf16[1,384,512]{2,1,0:T(8,128)(2,1)S(1)}, bf16[8,1,384,512]{3,2,1,0:T(8,128)(2,1)}, bf16[8,1,...) while((s32[]{:T(128)}, bf16[1,384,512]{2,1,0:T(8,128)(2,1)}, ...), condition=%wide.region_16.17_spmd, body=%wide.region_0.16_spmd.sunk | while | flops 10157273088 | bytes 302562272 | solution.py:134
  228.1 16.1 conditional.4
  254.2 16.1 conditional.4
  265.2 5.0 fusion.23
  278.1 49.4 %collective-permute-done.1 = bf16[1,384,512]{2,1,0:T(8,128)(2,1)S(1)} collective-permute-done((bf16[1,384,512]{2,1,0:T(8,128)(2,1)}, bf16[1,384,512]{2,1,0:T(8,128)(2,1)S(1)}, u32[]{:S(2)}, u32[]{:S(2)}) %collective-permute-start.1) | collective-permute-done | bytes 393248 | tf_op jit(solution)/shard_map/while/body/eval_jaxpr/ppermute | solution.py:130
  330.5 16.1 conditional.4
  341.5 5.0 fusion.23
  351.1 53.2 %conditional.5 = (bf16[1,384,512]{2,1,0:T(8,128)(2,1)}, f32[1,512,24,64]{1,3,2,0:T(8,128)}, f32[1,512,512]{2,1,0:T(8,128)}, f32[1,512,2048]{2,1,0:T(8,128)}, f32[1,2048,512]{2,1,0:T(8,128)}) conditional(s32[]{:T(128)} %convert_element_type.518, (f32[1,512,24,64]{1,3,2,0:T(8,128)}, f32[1,512,512]{2,1,0:T(8,128)}, f32[1,512,2048]{2,1,0:T(8,128)}, ...), branch_computations={%region_7.7_spmd, %region_8.15_spmd} | conditional | flops 7418964992 | bytes 267626400 | solution.py:128
  411.4 16.1 conditional.4
  422.4 5.0 fusion.23
  431.4 53.2 %conditional.5 = (bf16[1,384,512]{2,1,0:T(8,128)(2,1)}, f32[1,512,24,64]{1,3,2,0:T(8,128)}, f32[1,512,512]{2,1,0:T(8,128)}, f32[1,512,2048]{2,1,0:T(8,128)}, f32[1,2048,512]{2,1,0:T(8,128)}) conditional(s32[]{:T(128)} %convert_element_type.518, (f32[1,512,24,64]{1,3,2,0:T(8,128)}, f32[1,512,512]{2,1,0:T(8,128)}, f32[1,512,2048]{2,1,0:T(8,128)}, ...), branch_computations={%region_7.7_spmd, %region_8.15_spmd} | conditional | flops 7418964992 | bytes 267626400 | solution.py:128
  491.7 16.1 conditional.4
  511.7 53.2 %conditional.5 = (bf16[1,384,512]{2,1,0:T(8,128)(2,1)}, f32[1,512,24,64]{1,3,2,0:T(8,128)}, f32[1,512,512]{2,1,0:T(8,128)}, f32[1,512,2048]{2,1,0:T(8,128)}, f32[1,2048,512]{2,1,0:T(8,128)}) conditional(s32[]{:T(128)} %convert_element_type.518, (f32[1,512,24,64]{1,3,2,0:T(8,128)}, f32[1,512,512]{2,1,0:T(8,128)}, f32[1,512,2048]{2,1,0:T(8,128)}, ...), branch_computations={%region_7.7_spmd, %region_8.15_spmd} | conditional | flops 7418964992 | bytes 267626400 | solution.py:128
  572.0 16.1 conditional.4
  583.1 5.0 fusion.23
  592.0 53.2 %conditional.5 = (bf16[1,384,512]{2,1,0:T(8,128)(2,1)}, f32[1,512,24,64]{1,3,2,0:T(8,128)}, f32[1,512,512]{2,1,0:T(8,128)}, f32[1,512,2048]{2,1,0:T(8,128)}, f32[1,2048,512]{2,1,0:T(8,128)}) conditional(s32[]{:T(128)} %convert_element_type.518, (f32[1,512,24,64]{1,3,2,0:T(8,128)}, f32[1,512,512]{2,1,0:T(8,128)}, f32[1,512,2048]{2,1,0:T(8,128)}, ...), branch_computations={%region_7.7_spmd, %region_8.15_spmd} | conditional | flops 7418964992 | bytes 267626400 | solution.py:128
  652.3 16.1 conditional.4
  663.4 5.0 fusion.23
  672.3 53.2 %conditional.5 = (bf16[1,384,512]{2,1,0:T(8,128)(2,1)}, f32[1,512,24,64]{1,3,2,0:T(8,128)}, f32[1,512,512]{2,1,0:T(8,128)}, f32[1,512,2048]{2,1,0:T(8,128)}, f32[1,2048,512]{2,1,0:T(8,128)}) conditional(s32[]{:T(128)} %convert_element_type.518, (f32[1,512,24,64]{1,3,2,0:T(8,128)}, f32[1,512,512]{2,1,0:T(8,128)}, f32[1,512,2048]{2,1,0:T(8,128)}, ...), branch_computations={%region_7.7_spmd, %region_8.15_spmd} | conditional | flops 7418964992 | bytes 267626400 | solution.py:128
  732.7 16.1 conditional.4
  752.7 53.2 %conditional.5 = (bf16[1,384,512]{2,1,0:T(8,128)(2,1)}, f32[1,512,24,64]{1,3,2,0:T(8,128)}, f32[1,512,512]{2,1,0:T(8,128)}, f32[1,512,2048]{2,1,0:T(8,128)}, f32[1,2048,512]{2,1,0:T(8,128)}) conditional(s32[]{:T(128)} %convert_element_type.518, (f32[1,512,24,64]{1,3,2,0:T(8,128)}, f32[1,512,512]{2,1,0:T(8,128)}, f32[1,512,2048]{2,1,0:T(8,128)}, ...), branch_computations={%region_7.7_spmd, %region_8.15_spmd} | conditional | flops 7418964992 | bytes 267626400 | solution.py:128
  813.8 19.2 collective-permute-start
  833.0 53.2 %conditional.5 = (bf16[1,384,512]{2,1,0:T(8,128)(2,1)}, f32[1,512,24,64]{1,3,2,0:T(8,128)}, f32[1,512,512]{2,1,0:T(8,128)}, f32[1,512,2048]{2,1,0:T(8,128)}, f32[1,2048,512]{2,1,0:T(8,128)}) conditional(s32[]{:T(128)} %convert_element_type.518, (f32[1,512,24,64]{1,3,2,0:T(8,128)}, f32[1,512,512]{2,1,0:T(8,128)}, f32[1,512,2048]{2,1,0:T(8,128)}, ...), branch_computations={%region_7.7_spmd, %region_8.15_spmd} | conditional | flops 7418964992 | bytes 267626400 | solution.py:128
  898.0 53.2 %conditional.5 = (bf16[1,384,512]{2,1,0:T(8,128)(2,1)}, f32[1,512,24,64]{1,3,2,0:T(8,128)}, f32[1,512,512]{2,1,0:T(8,128)}, f32[1,512,2048]{2,1,0:T(8,128)}, f32[1,2048,512]{2,1,0:T(8,128)}) conditional(s32[]{:T(128)} %convert_element_type.518, (f32[1,512,24,64]{1,3,2,0:T(8,128)}, f32[1,512,512]{2,1,0:T(8,128)}, f32[1,512,2048]{2,1,0:T(8,128)}, ...), branch_computations={%region_7.7_spmd, %region_8.15_spmd} | conditional | flops 7418964992 | bytes 267626400 | solution.py:128
  954.9 5.9 copy.35
  966.0 341.7 %reduce-scatter.8.cloned.1.call-done = f32[1,8,512]{2,1,0:T(8,128)} async-done(((f32[1,512,512]{2,1,0:T(8,128)}), f32[1,8,512]{2,1,0:T(8,128)}) %reduce-scatter.8.cloned.1.call-update) | async-done | bytes 16400 | tf_op jit(solution)/shard_map/reduce_scatter | solution.py:136
  1307.7 226.7 %reduce-scatter.6.cloned.1.call-done = f32[1,8,24,64]{3,2,1,0:T(8,128)} async-done(((f32[1,512,24,64]{3,2,1,0:T(8,128)}), f32[1,8,24,64]{3,2,1,0:T(8,128)}) %reduce-scatter.6.cloned.1.call-update) | async-done | bytes 49168 | tf_op jit(solution)/shard_map/reduce_scatter | solution.py:136
  1534.5 12.9 reduce-scatter.14.cloned.1.call-done
  1547.4 365.4 %reduce-scatter.10.cloned.1.call-done = f32[1,8,2048]{2,1,0:T(8,128)} async-done(((f32[1,512,2048]{2,1,0:T(8,128)}), f32[1,8,2048]{2,1,0:T(8,128)}) %reduce-scatter.10.cloned.1.call-update) | async-done | bytes 65552 | tf_op jit(solution)/shard_map/reduce_scatter | solution.py:136
  1912.8 358.7 %reduce-scatter.12.cloned.1.call-done = f32[1,32,512]{2,1,0:T(8,128)} async-done(((f32[1,2048,512]{2,1,0:T(8,128)}), f32[1,32,512]{2,1,0:T(8,128)}) %reduce-scatter.12.cloned.1.call-update) | async-done | bytes 65552 | tf_op jit(solution)/shard_map/reduce_scatter | solution.py:136
  (911 shorter events, 660.3 us)
Async XLA Ops:
  7.2 183.5 %all-gather.4.cloned.1.call-start = ((), (), s32[]{:S(2)}) async-start(), calls=%async_computation.5 | async-start | bytes 3194880 | tf_op jit(solution)/shard_map/all_gather | solution.py:96
  7.9 187.4 %all-gather.6.cloned.1.call-start = ((), (), s32[]{:S(2)}) async-start(), calls=%async_computation.6 | async-start | bytes 2129920 | tf_op jit(solution)/shard_map/all_gather | solution.py:96
  8.6 203.5 %all-gather.8.cloned.1.call-start = ((), (), s32[]{:S(2)}) async-start(), calls=%async_computation.7 | async-start | bytes 2129920 | tf_op jit(solution)/shard_map/all_gather | solution.py:96
  9.4 1298.3 %reduce-scatter.8.cloned.1.call-start = ((), (), s32[]{:S(2)}) async-start(), calls=%async_computation.9 | async-start | bytes 1064960 | tf_op jit(solution)/shard_map/reduce_scatter | solution.py:136
  244.2 7.0 collective-permute-start
  247.0 4.2 collective-permute-start.1
  270.2 7.9 collective-permute-start
  274.0 53.5 %collective-permute-start.1 = (bf16[1,384,512]{2,1,0:T(8,128)(2,1)}, bf16[1,384,512]{2,1,0:T(8,128)(2,1)S(1)}, u32[]{:S(2)}, u32[]{:S(2)}) collective-permute-start(bf16[1,384,512]{2,1,0:T(8,128)(2,1)} %get-tuple-element.758), channel_id=1, source_target_pairs={{64,0},{65,1},{66,2},{67,3},{68,4},{69,5},{70,6},{71,7},{72,8},{73... | collective-permute-start | bytes 1179656 | tf_op jit(solution)/shard_map/while/body/eval_jaxpr/ppermute | solution.py:130
  346.5 61.9 %collective-permute-start = (bf16[1,384,512]{2,1,0:T(8,128)(2,1)}, bf16[1,384,512]{2,1,0:T(8,128)(2,1)}, u32[]{:S(2)}, u32[]{:S(2)}) collective-permute-start(bf16[1,384,512]{2,1,0:T(8,128)(2,1)} %get-tuple-element.842), channel_id=1, source_target_pairs={{0,64},{1,65},{2,66},{3,67},{4,68},{5,69},{6,70},{7,71},{8,72},{9,... | collective-permute-start | bytes 1179656 | tf_op jit(solution)/shard_map/while/body/eval_jaxpr/ppermute | solution.py:129
  357.5 7.2 copy-start.2
  404.2 4.2 collective-permute-start.1
  427.5 61.3 %collective-permute-start = (bf16[1,384,512]{2,1,0:T(8,128)(2,1)}, bf16[1,384,512]{2,1,0:T(8,128)(2,1)}, u32[]{:S(2)}, u32[]{:S(2)}) collective-permute-start(bf16[1,384,512]{2,1,0:T(8,128)(2,1)} %get-tuple-element.842), channel_id=1, source_target_pairs={{0,64},{1,65},{2,66},{3,67},{4,68},{5,69},{6,70},{7,71},{8,72},{9,... | collective-permute-start | bytes 1179656 | tf_op jit(solution)/shard_map/while/body/eval_jaxpr/ppermute | solution.py:129
  484.6 4.2 collective-permute-start.1
  507.8 61.3 %collective-permute-start = (bf16[1,384,512]{2,1,0:T(8,128)(2,1)}, bf16[1,384,512]{2,1,0:T(8,128)(2,1)}, u32[]{:S(2)}, u32[]{:S(2)}) collective-permute-start(bf16[1,384,512]{2,1,0:T(8,128)(2,1)} %get-tuple-element.842), channel_id=1, source_target_pairs={{0,64},{1,65},{2,66},{3,67},{4,68},{5,69},{6,70},{7,71},{8,72},{9,... | collective-permute-start | bytes 1179656 | tf_op jit(solution)/shard_map/while/body/eval_jaxpr/ppermute | solution.py:129
  564.9 4.2 collective-permute-start.1
  588.1 61.3 %collective-permute-start = (bf16[1,384,512]{2,1,0:T(8,128)(2,1)}, bf16[1,384,512]{2,1,0:T(8,128)(2,1)}, u32[]{:S(2)}, u32[]{:S(2)}) collective-permute-start(bf16[1,384,512]{2,1,0:T(8,128)(2,1)} %get-tuple-element.842), channel_id=1, source_target_pairs={{0,64},{1,65},{2,66},{3,67},{4,68},{5,69},{6,70},{7,71},{8,72},{9,... | collective-permute-start | bytes 1179656 | tf_op jit(solution)/shard_map/while/body/eval_jaxpr/ppermute | solution.py:129
  645.2 4.2 collective-permute-start.1
  668.4 61.3 %collective-permute-start = (bf16[1,384,512]{2,1,0:T(8,128)(2,1)}, bf16[1,384,512]{2,1,0:T(8,128)(2,1)}, u32[]{:S(2)}, u32[]{:S(2)}) collective-permute-start(bf16[1,384,512]{2,1,0:T(8,128)(2,1)} %get-tuple-element.842), channel_id=1, source_target_pairs={{0,64},{1,65},{2,66},{3,67},{4,68},{5,69},{6,70},{7,71},{8,72},{9,... | collective-permute-start | bytes 1179656 | tf_op jit(solution)/shard_map/while/body/eval_jaxpr/ppermute | solution.py:129
  678.8 7.2 copy-start.2
  725.5 4.2 collective-permute-start.1
  748.7 61.3 %collective-permute-start = (bf16[1,384,512]{2,1,0:T(8,128)(2,1)}, bf16[1,384,512]{2,1,0:T(8,128)(2,1)}, u32[]{:S(2)}, u32[]{:S(2)}) collective-permute-start(bf16[1,384,512]{2,1,0:T(8,128)(2,1)} %get-tuple-element.842), channel_id=1, source_target_pairs={{0,64},{1,65},{2,66},{3,67},{4,68},{5,69},{6,70},{7,71},{8,72},{9,... | collective-permute-start | bytes 1179656 | tf_op jit(solution)/shard_map/while/body/eval_jaxpr/ppermute | solution.py:129
  805.8 4.2 collective-permute-start.1
  813.8 75.6 %collective-permute-start = (bf16[1,384,512]{2,1,0:T(8,128)(2,1)}, bf16[1,384,512]{2,1,0:T(8,128)(2,1)}, u32[]{:S(2)}, u32[]{:S(2)}) collective-permute-start(bf16[1,384,512]{2,1,0:T(8,128)(2,1)} %get-tuple-element.842), channel_id=1, source_target_pairs={{0,64},{1,65},{2,66},{3,67},{4,68},{5,69},{6,70},{7,71},{8,72},{9,... | collective-permute-start | bytes 1179656 | tf_op jit(solution)/shard_map/while/body/eval_jaxpr/ppermute | solution.py:129
  839.4 7.2 copy-start.2
  886.2 3.6 collective-permute-start.1
  893.5 60.9 %collective-permute-start = (bf16[1,384,512]{2,1,0:T(8,128)(2,1)}, bf16[1,384,512]{2,1,0:T(8,128)(2,1)}, u32[]{:S(2)}, u32[]{:S(2)}) collective-permute-start(bf16[1,384,512]{2,1,0:T(8,128)(2,1)} %get-tuple-element.842), channel_id=1, source_target_pairs={{0,64},{1,65},{2,66},{3,67},{4,68},{5,69},{6,70},{7,71},{8,72},{9,... | collective-permute-start | bytes 1179656 | tf_op jit(solution)/shard_map/while/body/eval_jaxpr/ppermute | solution.py:129
  904.4 7.2 copy-start.2
  951.2 3.6 collective-permute-start.1
  954.8 579.7 %reduce-scatter.6.cloned.1.call-start = ((), (), s32[]{:S(2)}) async-start(), calls=%async_computation.8 | async-start | bytes 6389760 | tf_op jit(solution)/shard_map/reduce_scatter | solution.py:136
  960.8 586.6 %reduce-scatter.14.cloned.1.call-start = ((), (), s32[]{:S(2)}) async-start(), calls=%async_computation.12 | async-start | bytes 4718592 | tf_op jit(solution)/shard_map/reduce_scatter | solution.py:138
  964.5 948.3 %reduce-scatter.10.cloned.1.call-start = ((), (), s32[]{:S(2)}) async-start(), calls=%async_computation.10 | async-start | bytes 4259840 | tf_op jit(solution)/shard_map/reduce_scatter | solution.py:136
  965.3 1306.3 %reduce-scatter.12.cloned.1.call-start = ((), (), s32[]{:S(2)}) async-start(), calls=%async_computation.11 | async-start | bytes 4259840 | tf_op jit(solution)/shard_map/reduce_scatter | solution.py:136
  (221 other events, 634.7 us)
Sparse Core Ops, SparseCore 0:
  10.7 69.6 all-gather.3
  83.3 63.0 all-gather.5
  149.2 62.8 all-gather.7
  954.9 352.7 reduce-scatter.7
  1312.6 221.8 reduce-scatter.5
  1537.3 10.0 reduce-scatter.13
  1550.3 362.4 reduce-scatter.9
  1915.7 355.7 reduce-scatter.11
where the time goes:
time: 2280 us
  waiting for transfers between devices  1380 us (61%)
  matrix products  380 us (17%)
  blocking collectives  181 us (8%)
  other arithmetic  146 us (6%)
  local copies, waits for them, and re-layouts  111 us (5%)
  starting transfers between devices  66 us (3%)
    reduce_scatter x4, waiting for transfers between devices, device_step(): lax.psum_scatter(acc_part, 'dp', scatter_dimension=1, tiled=True)  1290 us
    all_gather x1, blocking collectives, device_step(): lax.all_gather(w_part, 'dp', axis=1, tiled=True)  181 us
    dot_general x32, matrix products, attn_core(): jnp.einsum('bnqk,bknh->bqnh', prob_bf, v_heads, preferred_element_type=jn...  65 us
    sub x16, matrix products, attn_core(): jax.nn.softmax(jnp.where(causal, scores, -1e+30), axis=-1)  60.8 us
    cond x24, matrix products  57.2 us
    ppermute x10, starting transfers between devices, run_tick(): fwd_buf = lax.ppermute(stage_out, 'pp', fwd_pairs)  52.8 us
    cond x448, local copies, waits for them, and re-layouts  52.2 us
    ppermute x10, waiting for transfers between devices, run_tick(): bwd_buf = lax.ppermute(ct_in, 'pp', bwd_pairs)  50.2 us
  transfers between devices with their start and end apart: 28, of which 9 were waited for; matrix products, arithmetic and copies ran while one was open for 18% of the time, Pallas kernels for 0%

commit v1 on v0

v1 whole, which is shorter than its diff:
```python
import functools

import jax
import jax.numpy as jnp
from jax import lax
from jax.experimental import pallas as pl
from jax.experimental.pallas import tpu as pltpu
from jax.sharding import Mesh
from jax.sharding import PartitionSpec as P

NORM_EPS = 1e-6
BF = jnp.bfloat16
F32 = jnp.float32


def rms_norm(hidden):
    return hidden * lax.rsqrt(jnp.mean(hidden * hidden, axis=-1, keepdims=True) + NORM_EPS)


def gelu_tanh(pre_act):
    return jax.nn.gelu(pre_act, approximate=True)


def dot(a, b):
    return lax.dot_general(a, b, (((1,), (0,)), ((), ())), preferred_element_type=F32)


def dot_nt(a, b):
    return lax.dot_general(a, b, (((1,), (1,)), ((), ())), preferred_element_type=F32)


def dot_tn(a, b):
    return lax.dot_general(a, b, (((0,), (0,)), ((), ())), preferred_element_type=F32)


def softmax_rows(q, kh, scale):
    s = dot_nt(q, kh) * scale
    row = lax.broadcasted_iota(jnp.int32, s.shape, 0)
    col = lax.broadcasted_iota(jnp.int32, s.shape, 1)
    s = jnp.where(row >= col, s, -1e30)
    e = jnp.exp(s - jnp.max(s, axis=-1, keepdims=True))
    return e * (1.0 / jnp.sum(e, axis=-1, keepdims=True))


def attn_fwd_kernel(scale, q_ref, k_ref, v_ref, o_ref):
    q, k, v = q_ref[...], k_ref[...], v_ref[...]
    low = lax.broadcasted_iota(jnp.int32, k.shape, 1) < 64
    zero = jnp.zeros_like(k)
    out = jnp.zeros(q.shape, F32)
    for half in range(2):
        keep = low if half == 0 else jnp.logical_not(low)
        p = softmax_rows(q, jnp.where(keep, k, zero), scale).astype(BF)
        out = out + dot(p, jnp.where(keep, v, zero))
    o_ref[...] = out.astype(BF)


def attn_bwd_kernel(scale, width, q_ref, k_ref, v_ref, do_ref, dqkv_ref):
    q, k, v, do = q_ref[...], k_ref[...], v_ref[...], do_ref[...]
    low = lax.broadcasted_iota(jnp.int32, k.shape, 1) < 64
    zero = jnp.zeros_like(k)
    dq = jnp.zeros(q.shape, F32)
    dk = jnp.zeros(q.shape, F32)
    dv = jnp.zeros(q.shape, F32)
    for half in range(2):
        keep = low if half == 0 else jnp.logical_not(low)
        kh, vh = jnp.where(keep, k, zero), jnp.where(keep, v, zero)
        qh, doh = jnp.where(keep, q, zero), jnp.where(keep, do, zero)
        p = softmax_rows(q, kh, scale)
        dp = dot_nt(do, vh).astype(BF).astype(F32)
        delta = jnp.sum(dp * p, axis=-1, keepdims=True)
        ds = (p * (dp - delta) * scale).astype(BF)
        dq = dq + dot(ds, kh)
        dk = dk + dot_tn(ds, qh)
        dv = dv + dot_tn(p.astype(BF), doh)
    base = pl.program_id(1) * 128
    dqkv_ref[:, pl.ds(pl.multiple_of(base, 128), 128)] = dq.astype(BF)
    dqkv_ref[:, pl.ds(pl.multiple_of(base + width, 128), 128)] = dk.astype(BF)
    dqkv_ref[:, pl.ds(pl.multiple_of(base + 2 * width, 128), 128)] = dv.astype(BF)


def attn_fwd(qkv, seq, scale):
    tokens, width = qkv.shape[0], qkv.shape[1] // 3
    pairs = width // 128
    spec = lambda off: pl.BlockSpec((seq, 128), lambda b, j: (b, off + j))
    return pl.pallas_call(
        functools.partial(attn_fwd_kernel, scale),
        grid=(tokens // seq, pairs),
        in_specs=[spec(0), spec(pairs), spec(2 * pairs)],
        out_specs=spec(0),
        out_shape=jax.ShapeDtypeStruct((tokens, width), BF),
        cost_estimate=pl.CostEstimate(flops=int(2e10), bytes_accessed=4 * tokens * width * 2, transcendentals=0),
        name="attn_fwd",
    )(qkv, qkv, qkv)


def attn_bwd(qkv, do, seq, scale):
    tokens, width = qkv.shape[0], qkv.shape[1] // 3
    pairs = width // 128
    spec = lambda off: pl.BlockSpec((seq, 128), lambda b, j: (b, off + j))
    return pl.pallas_call(
        functools.partial(attn_bwd_kernel, scale, width),
        grid=(tokens // seq, pairs),
        in_specs=[spec(0), spec(pairs), spec(2 * pairs), spec(0)],
        out_specs=pl.BlockSpec((seq, 3 * width), lambda b, j: (b, 0)),
        out_shape=jax.ShapeDtypeStruct((tokens, 3 * width), BF),
        cost_estimate=pl.CostEstimate(flops=int(5e10), bytes_accessed=7 * tokens * width * 2, transcendentals=0),
        name="attn_bwd",
    )(qkv, qkv, qkv, do)


def layer_forward(hidden, weights, seq, scale):
    w_qkv, w_proj, w_up, w_down = weights
    hid_f32 = hidden.astype(F32)
    normed = rms_norm(hid_f32).astype(BF)
    qkv = dot(normed, w_qkv).astype(BF)
    attn = attn_fwd(qkv, seq, scale)
    mid = (hid_f32 + dot(attn, w_proj)).astype(BF)
    mid_f32 = mid.astype(F32)
    normed2 = rms_norm(mid_f32).astype(BF)
    up = dot(normed2, w_up).astype(BF)
    gelu = gelu_tanh(up.astype(F32)).astype(BF)
    out = (mid_f32 + dot(gelu, w_down)).astype(BF)
    return out, (hidden, normed, qkv, attn, mid, normed2, up, gelu)


def layer_backward(saved, ct_out, weights, seq, scale, need_input):
    w_qkv, w_proj, w_up, w_down = weights
    hidden, normed, qkv, attn, mid, normed2, up, gelu = saved
    g_down = dot_tn(gelu, ct_out)
    ct_gelu = dot_nt(ct_out, w_down).astype(BF)
    ct_up = jax.vjp(gelu_tanh, up.astype(F32))[1](ct_gelu.astype(F32))[0].astype(BF)
    g_up = dot_tn(normed2, ct_up)
    ct_norm2 = dot_nt(ct_up, w_up).astype(BF)
    ct_mid = (ct_out.astype(F32) + jax.vjp(rms_norm, mid.astype(F32))[1](ct_norm2.astype(F32))[0]).astype(BF)
    g_proj = dot_tn(attn, ct_mid)
    ct_attn = dot_nt(ct_mid, w_proj).astype(BF)
    ct_qkv = attn_bwd(qkv, ct_attn, seq, scale)
    g_qkv = dot_tn(normed, ct_qkv)
    ct_hidden = None
    if need_input:
        ct_norm = dot_nt(ct_qkv, w_qkv).astype(BF)
        ct_hidden = (ct_mid.astype(F32) + jax.vjp(rms_norm, hidden.astype(F32))[1](ct_norm.astype(F32))[0]).astype(BF)
    return ct_hidden, (g_qkv, g_proj, g_up, g_down)


def solution(mesh):
    stages = mesh.shape['pp']
    grid = Mesh(mesh.devices.reshape(2, 4, 4, 4), ("pp", "z", "y", "x"))
    dp = ("z", "y", "x")
    swap = [(0, 1), (1, 0)]

    def device_step(act_in, loss_seed, w_qkv, w_proj, w_up, w_down):
        micro, _, seq, d = act_in.shape
        mine = micro // 2
        pp = lax.axis_index('pp')
        heads3, hd = w_qkv.shape[2:]
        scale = hd ** -0.5

        def gather(w):
            flat = w.reshape(w.shape[1], -1)
            full = lax.all_gather(flat, ("pp",) + dp, axis=0, tiled=True)
            return full.reshape(2, full.shape[0] // 2, full.shape[1])

        full = [gather(w) for w in (w_qkv, w_proj, w_up, w_down)]
        layers = [[w[i] for w in full] for i in range(2)]
        act = lax.dynamic_slice_in_dim(act_in, pp * mine, mine, 0).reshape(mine * seq, d)
        seed = lax.dynamic_slice_in_dim(loss_seed, pp * mine, mine, 0).reshape(mine * seq, d)
        h1, saved0 = layer_forward(act, layers[0], seq, scale)
        h2, saved1 = layer_forward(h1, layers[1], seq, scale)

        out4 = h2.reshape(mine, 1, seq, d)
        half = seq // 2
        keep = lax.dynamic_slice_in_dim(out4, pp * half, half, 2)
        give = lax.dynamic_slice_in_dim(out4, (1 - pp) * half, half, 2)
        got = lax.ppermute(give, 'pp', swap)
        act_out = jnp.concatenate([jnp.where(pp == 0, keep, got), jnp.where(pp == 0, got, keep)], axis=0)

        ct1, grads1 = layer_backward(saved1, seed, layers[1], seq, scale, True)
        _, grads0 = layer_backward(saved0, ct1, layers[0], seq, scale, False)

        def reduce(g):
            rows, cols = g.shape
            h = cols // 2
            keep = lax.dynamic_slice_in_dim(g, pp * h, h, 1)
            give = lax.dynamic_slice_in_dim(g, (1 - pp) * h, h, 1)
            part = keep + lax.ppermute(give, 'pp', swap)
            for axis in dp:
                part = lax.psum_scatter(part, axis, scatter_dimension=0, tiled=True)
            return part

        def finish(p0, p1):
            keep = jnp.where(pp == 0, p0, p1)
            give = jnp.where(pp == 0, p1, p0)
            got = lax.ppermute(give, 'pp', swap)
            return jnp.concatenate([jnp.where(pp == 0, keep, got), jnp.where(pp == 0, got, keep)], axis=1)

        red1 = [reduce(g) for g in grads1]
        red0 = [reduce(g) for g in grads0]
        outs = [finish(a, b) for a, b in zip(red0, red1)]
        return tuple(o.reshape(w.shape) for o, w in zip(outs, (w_qkv, w_proj, w_up, w_down))) + (act_out,)

    weight_spec = P('pp', dp)
    act_spec = P(None, dp)
    return jax.shard_map(device_step, mesh=grid, in_specs=(act_spec, act_spec) + (weight_spec,) * 4, out_specs=(weight_spec,) * 4 + (P(None, dp, 'pp'),), check_vma=False)
```

time: 2280 us -> 1000 us (0.44)
  the two profiles are of different devices: /device:TPU:0 before, /device:TPU:1 now
where the time goes in v1:
time: 1000 us; the launch traced here: 999 us
  waiting for transfers between devices  687 us (69%)
  matrix products  125 us (12%)
  Pallas kernels  84.9 us (8%)
  other arithmetic  46.1 us (5%)
  local copies, waits for them, and re-layouts  23.3 us (2%)
  starting transfers between devices  16.3 us (2%)
  between operations  15.5 us (2%)
    reduce_scatter x24, waiting for transfers between devices, reduce(): part = lax.psum_scatter(part, axis, scatter_dimension=0, tiled=True)  440 us
    all_gather x4, waiting for transfers between devices, gather(): full = lax.all_gather(flat, ('pp',) + dp, axis=0, tiled=True)  226 us
    pallas_call x2, Pallas kernels, attn_bwd(): pl.pallas_call(functools.partial(attn_bwd_kernel, scale, width), grid=(to...  51.7 us
    dot_general x8, matrix products, dot(): lax.dot_general(a, b, (((1,), (0,)), ((), ())), preferred_element_type=F32)  44.5 us
    dot_general x8, matrix products, dot_tn(): lax.dot_general(a, b, (((0,), (0,)), ((), ())), preferred_element_type=F32)  41.9 us
    dot_general x7, matrix products, dot_nt(): lax.dot_general(a, b, (((1,), (1,)), ((), ())), preferred_element_type=F32)  38.9 us
    pallas_call x2, Pallas kernels, attn_fwd(): pl.pallas_call(functools.partial(attn_fwd_kernel, scale), grid=(tokens //...  33.2 us
    add x8, other arithmetic, reduce(): part = keep + lax.ppermute(give, 'pp', swap)  24.2 us
  transfers between devices with their start and end apart: 41, of which 30 were waited for; matrix products, arithmetic and copies ran while one was open for 14% of the time, Pallas kernels for 7%

profile of v1, /device:TPU:1, one launch (start us, length us, event | category | flops | bytes accessed | tf_op | source)
XLA Modules:
  0.0 998.7 jit_solution(11500371455173099926)
XLA Ops:
  16.8 64.1 %all-gather.8.cloned.1.call-done = bf16[1024,1536]{1,0:T(8,128)(2,1)} async-done(((bf16[8,1536]{1,0:T(8,128)(2,1)}), bf16[1024,1536]{1,0:T(8,128)(2,1)}) %all-gather.8.cloned.1.call-update) | async-done | bytes 3145744 | tf_op jit(solution)/shard_map/all_gather | solution.py:161
  87.7 16.6 %attn_fwd.2 = bf16[1536,512]{1,0:T(8,128)(2,1)} custom-call(bf16[1536,1536]{1,0:T(8,128)(2,1)} %convolution_convert_fusion.5.q_ref.k_ref.v_ref, bf16[1536,1536]{1,0:T(8,128)(2,1)} %convolution_convert_fusion.5.q_ref.k_ref.v_ref, bf16[1536,1536]{1,0:T(8,128)(2,1)} %convolution_convert_fusion.5.q_ref.k_ref.v_ref), custom_call_target="tpu_custom_call" | custom-call | flops 20000000000 | bytes 6291456 | tf_op jit(solution)/shard_map/attn_fwd/pallas_call | solution.py:85
  104.3 40.5 %all-gather.12.cloned.1.call-done = bf16[1,1024,512]{2,1,0:T(8,128)(2,1)} async-done(((bf16[1,8,512]{2,1,0:T(8,128)(2,1)}), bf16[1,1024,512]{2,1,0:T(8,128)(2,1)}) %all-gather.12.cloned.1.call-update) | async-done | bytes 1048592 | tf_op jit(solution)/shard_map/all_gather | solution.py:161
  149.1 63.1 %all-gather.14.cloned.1.call-done = bf16[1,1024,2048]{2,1,0:T(8,128)(2,1)} async-done(((bf16[1,8,2048]{2,1,0:T(8,128)(2,1)}), bf16[1,1024,2048]{2,1,0:T(8,128)(2,1)}) %all-gather.14.cloned.1.call-update) | async-done | bytes 4194320 | tf_op jit(solution)/shard_map/all_gather | solution.py:161
  212.2 8.3 convolution_convert_fusion.3
  220.5 58.8 %all-gather.10.cloned.1.call-done = bf16[1,4096,512]{2,1,0:T(8,128)(2,1)} async-done(((bf16[1,32,512]{2,1,0:T(8,128)(2,1)}), bf16[1,4096,512]{2,1,0:T(8,128)(2,1)}) %all-gather.10.cloned.1.call-update) | async-done | bytes 4194320 | tf_op jit(solution)/shard_map/all_gather | solution.py:161
  291.4 16.6 %attn_fwd.3 = bf16[1536,512]{1,0:T(8,128)(2,1)} custom-call(bf16[1536,1536]{1,0:T(8,128)(2,1)} %convolution_convert_fusion.2.q_ref.k_ref.v_ref, bf16[1536,1536]{1,0:T(8,128)(2,1)} %convolution_convert_fusion.2.q_ref.k_ref.v_ref, bf16[1536,1536]{1,0:T(8,128)(2,1)} %convolution_convert_fusion.2.q_ref.k_ref.v_ref), custom_call_target="tpu_custom_call" | custom-call | flops 20000000000 | bytes 6291456 | tf_op jit(solution)/shard_map/attn_fwd/pallas_call | solution.py:85
  314.5 11.4 %fusion.4 = bf16[1536,2048]{1,0:T(8,128)(2,1)S(1)} fusion(bf16[1536,2048]{1,0:T(8,128)(2,1)S(1)} %convolution_convert_fusion.1, bf16[1536,512]{1,0:T(8,128)(2,1)S(1)} %bitcast.75, bf16[1,4096,512]{2,1,0:T(8,128)(2,1)S(1)} %copy-done.40), kind=kOutput, calls=%fused_computation.16 | convolution fusion | flops 3293577216 | bytes 16252928 | tf_op jit(solution)/shard_map/dot_general | solution.py:29
  335.5 26.0 %attn_bwd.2 = bf16[1536,1536]{1,0:T(8,128)(2,1)} custom-call(bf16[1536,1536]{1,0:T(8,128)(2,1)} %convolution_convert_fusion.2.q_ref.k_ref.v_ref, bf16[1536,1536]{1,0:T(8,128)(2,1)} %convolution_convert_fusion.2.q_ref.k_ref.v_ref, bf16[1536,1536]{1,0:T(8,128)(2,1)} %convolution_convert_fusion.2.q_ref.k_ref.v_ref, ...), custom_call_target="tpu_custom_call" | custom-call | flops 49999998976 | bytes 11010048 | tf_op jit(solution)/shard_map/attn_bwd/pallas_call | solution.py:100
  374.0 11.3 %fusion.7 = bf16[1536,2048]{1,0:T(8,128)(2,1)S(1)} fusion(bf16[1536,2048]{1,0:T(8,128)(2,1)S(1)} %bitcast.81, bf16[1536,512]{1,0:T(8,128)(2,1)S(1)} %fusion.25, bf16[1,4096,512]{2,1,0:T(8,128)(2,1)S(1)} %copy-done.41), kind=kOutput, calls=%fused_computation.19 | convolution fusion | flops 3293577216 | bytes 16252928 | tf_op jit(solution)/shard_map/dot_general | solution.py:29
  408.0 25.7 %attn_bwd.3 = bf16[1536,1536]{1,0:T(8,128)(2,1)} custom-call(bf16[1536,1536]{1,0:T(8,128)(2,1)} %convolution_convert_fusion.5.q_ref.k_ref.v_ref, bf16[1536,1536]{1,0:T(8,128)(2,1)} %convolution_convert_fusion.5.q_ref.k_ref.v_ref, bf16[1536,1536]{1,0:T(8,128)(2,1)} %convolution_convert_fusion.5.q_ref.k_ref.v_ref, ...), custom_call_target="tpu_custom_call" | custom-call | flops 49999998976 | bytes 11010048 | tf_op jit(solution)/shard_map/attn_bwd/pallas_call | solution.py:100
  481.9 7.7 fusion.58
  515.3 8.8 reduce-scatter.55.cloned.1.call-done
  524.2 20.4 %reduce-scatter.45.cloned.1.call-done = f32[32,256]{1,0:T(8,128)} async-done(((f32[128,256]{1,0:T(8,128)}), f32[32,256]{1,0:T(8,128)}) %reduce-scatter.45.cloned.1.call-update) | async-done | bytes 32784 | tf_op jit(solution)/shard_map/reduce_scatter | solution.py:188
  544.7 22.7 %reduce-scatter.39.cloned.1.call-done = f32[32,256]{1,0:T(8,128)} async-done(((f32[128,256]{1,0:T(8,128)}), f32[32,256]{1,0:T(8,128)}) %reduce-scatter.39.cloned.1.call-update) | async-done | bytes 32784 | tf_op jit(solution)/shard_map/reduce_scatter | solution.py:188
  567.5 33.9 %reduce-scatter.49.cloned.1.call-done = f32[128,1024]{1,0:T(8,128)} async-done(((f32[512,1024]{1,0:T(8,128)}), f32[128,1024]{1,0:T(8,128)}) %reduce-scatter.49.cloned.1.call-update) | async-done | bytes 524304 | tf_op jit(solution)/shard_map/reduce_scatter | solution.py:188
  601.4 20.9 %reduce-scatter.33.cloned.1.call-done = f32[32,768]{1,0:T(8,128)} async-done(((f32[128,768]{1,0:T(8,128)}), f32[32,768]{1,0:T(8,128)}) %reduce-scatter.33.cloned.1.call-update) | async-done | bytes 98320 | tf_op jit(solution)/shard_map/reduce_scatter | solution.py:188
  622.7 22.7 %reduce-scatter.27.cloned.1.call-done = f32[32,768]{1,0:T(8,128)} async-done(((f32[128,768]{1,0:T(8,128)}), f32[32,768]{1,0:T(8,128)}) %reduce-scatter.27.cloned.1.call-update) | async-done | bytes 98320 | tf_op jit(solution)/shard_map/reduce_scatter | solution.py:188
  645.5 33.9 %reduce-scatter.67.cloned.1.call-done = f32[512,256]{1,0:T(8,128)} async-done(((f32[2048,256]{1,0:T(8,128)}), f32[512,256]{1,0:T(8,128)}) %reduce-scatter.67.cloned.1.call-update) | async-done | bytes 524304 | tf_op jit(solution)/shard_map/reduce_scatter | solution.py:188
  689.0 22.2 %reduce-scatter.61.cloned.1.call-done = f32[512,256]{1,0:T(8,128)} async-done(((f32[2048,256]{1,0:T(8,128)}), f32[512,256]{1,0:T(8,128)}) %reduce-scatter.61.cloned.1.call-update) | async-done | bytes 524304 | tf_op jit(solution)/shard_map/reduce_scatter | solution.py:188
  714.3 18.1 %reduce-scatter.57.cloned.1.call-done = f32[32,1024]{1,0:T(8,128)} async-done(((f32[128,1024]{1,0:T(8,128)}), f32[32,1024]{1,0:T(8,128)}) %reduce-scatter.57.cloned.1.call-update) | async-done | bytes 131088 | tf_op jit(solution)/shard_map/reduce_scatter | solution.py:188
  732.5 22.6 %reduce-scatter.47.cloned.1.call-done = f32[8,256]{1,0:T(8,128)} async-done(((f32[32,256]{1,0:T(8,128)}), f32[8,256]{1,0:T(8,128)}) %reduce-scatter.47.cloned.1.call-update) | async-done | bytes 8208 | tf_op jit(solution)/shard_map/reduce_scatter | solution.py:188
  755.1 22.6 %reduce-scatter.41.cloned.1.call-done = f32[8,256]{1,0:T(8,128)} async-done(((f32[32,256]{1,0:T(8,128)}), f32[8,256]{1,0:T(8,128)}) %reduce-scatter.41.cloned.1.call-update) | async-done | bytes 8208 | tf_op jit(solution)/shard_map/reduce_scatter | solution.py:188
  784.0 17.1 %reduce-scatter.51.cloned.1.call-done = f32[32,1024]{1,0:T(8,128)} async-done(((f32[128,1024]{1,0:T(8,128)}), f32[32,1024]{1,0:T(8,128)}) %reduce-scatter.51.cloned.1.call-update) | async-done | bytes 131088 | tf_op jit(solution)/shard_map/reduce_scatter | solution.py:188
  801.2 22.9 %reduce-scatter.35.cloned.1.call-done = f32[8,768]{1,0:T(8,128)} async-done(((f32[32,768]{1,0:T(8,128)}), f32[8,768]{1,0:T(8,128)}) %reduce-scatter.35.cloned.1.call-update) | async-done | bytes 24592 | tf_op jit(solution)/shard_map/reduce_scatter | solution.py:188
  824.1 22.7 %reduce-scatter.29.cloned.1.call-done = f32[8,768]{1,0:T(8,128)} async-done(((f32[32,768]{1,0:T(8,128)}), f32[8,768]{1,0:T(8,128)}) %reduce-scatter.29.cloned.1.call-update) | async-done | bytes 24592 | tf_op jit(solution)/shard_map/reduce_scatter | solution.py:188
  850.5 19.9 %reduce-scatter.69.cloned.1.call-done = f32[128,256]{1,0:T(8,128)} async-done(((f32[512,256]{1,0:T(8,128)}), f32[128,256]{1,0:T(8,128)}) %reduce-scatter.69.cloned.1.call-update) | async-done | bytes 131088 | tf_op jit(solution)/shard_map/reduce_scatter | solution.py:188
  871.8 22.3 %reduce-scatter.63.cloned.1.call-done = f32[128,256]{1,0:T(8,128)} async-done(((f32[512,256]{1,0:T(8,128)}), f32[128,256]{1,0:T(8,128)}) %reduce-scatter.63.cloned.1.call-update) | async-done | bytes 131088 | tf_op jit(solution)/shard_map/reduce_scatter | solution.py:188
  894.8 22.3 %reduce-scatter.59.cloned.1.call-done = f32[8,1024]{1,0:T(8,128)} async-done(((f32[32,1024]{1,0:T(8,128)}), f32[8,1024]{1,0:T(8,128)}) %reduce-scatter.59.cloned.1.call-update) | async-done | bytes 32784 | tf_op jit(solution)/shard_map/reduce_scatter | solution.py:188
  917.1 22.6 %reduce-scatter.53.cloned.1.call-done = f32[8,1024]{1,0:T(8,128)} async-done(((f32[32,1024]{1,0:T(8,128)}), f32[8,1024]{1,0:T(8,128)}) %reduce-scatter.53.cloned.1.call-update) | async-done | bytes 32784 | tf_op jit(solution)/shard_map/reduce_scatter | solution.py:188
  943.4 18.9 %reduce-scatter.71.cloned.1.call-done = f32[32,256]{1,0:T(8,128)} async-done(((f32[128,256]{1,0:T(8,128)}), f32[32,256]{1,0:T(8,128)}) %reduce-scatter.71.cloned.1.call-update) | async-done | bytes 32784 | tf_op jit(solution)/shard_map/reduce_scatter | solution.py:188
  962.3 22.7 %reduce-scatter.65.cloned.1.call-done = f32[32,256]{1,0:T(8,128)} async-done(((f32[128,256]{1,0:T(8,128)}), f32[32,256]{1,0:T(8,128)}) %reduce-scatter.65.cloned.1.call-update) | async-done | bytes 32784 | tf_op jit(solution)/shard_map/reduce_scatter | solution.py:188
  (259 shorter events, 192.8 us)
Async XLA Ops:
  7.2 73.8 %all-gather.8.cloned.1.call-start = ((), (), s32[]{:S(2)}) async-start(), calls=%async_computation.24 | async-start | bytes 3170304 | tf_op jit(solution)/shard_map/all_gather | solution.py:161
  8.9 135.9 %all-gather.12.cloned.1.call-start = ((), (), s32[]{:S(2)}) async-start(), calls=%async_computation.50 | async-start | bytes 1056768 | tf_op jit(solution)/shard_map/all_gather | solution.py:161
  9.7 202.5 %all-gather.14.cloned.1.call-start = ((), (), s32[]{:S(2)}) async-start(), calls=%async_computation.51 | async-start | bytes 4227072 | tf_op jit(solution)/shard_map/all_gather | solution.py:161
  10.4 268.9 %all-gather.10.cloned.1.call-start = ((), (), s32[]{:S(2)}) async-start(), calls=%async_computation.49 | async-start | bytes 4227072 | tf_op jit(solution)/shard_map/all_gather | solution.py:161
  11.0 462.9 %reduce-scatter.43.cloned.1.call-start = ((), (), s32[]{:S(2)}) async-start(), calls=%async_computation.34 | async-start | bytes 655360 | tf_op jit(solution)/shard_map/reduce_scatter | solution.py:188
  333.1 57.4 %collective-permute-start.4 = (f32[512,256]{1,0:T(8,128)}, f32[512,256]{1,0:T(8,128)}, u32[]{:S(2)}, u32[]{:S(2)}) collective-permute-start(f32[512,256]{1,0:T(8,128)} %constant_dynamic-slice_fusion.5), channel_id=1, source_target_pairs={{0,64},{64,0},{1,65},{65,1},{2,66},{66,2},{3,67},{67,3},{4,68},{68... | collective-permute-start | bytes 1572872 | tf_op jit(solution)/shard_map/ppermute | solution.py:186
  393.0 80.9 %reduce-scatter.37.cloned.1.call-start = ((), (), s32[]{:S(2)}) async-start(), calls=%async_computation.31 | async-start | bytes 655360 | tf_op jit(solution)/shard_map/reduce_scatter | solution.py:188
  399.9 93.5 %reduce-scatter.31.cloned.1.call-start = ((), (), s32[]{:S(2)}) async-start(), calls=%async_computation.28 | async-start | bytes 1966080 | tf_op jit(solution)/shard_map/reduce_scatter | solution.py:188
  408.0 85.5 %reduce-scatter.25.cloned.1.call-start = ((), (), s32[]{:S(2)}) async-start(), calls=%async_computation.25 | async-start | bytes 1966080 | tf_op jit(solution)/shard_map/reduce_scatter | solution.py:188
  446.2 77.9 %reduce-scatter.55.cloned.1.call-start = ((), (), s32[]{:S(2)}) async-start(), calls=%async_computation.40 | async-start | bytes 2621440 | tf_op jit(solution)/shard_map/reduce_scatter | solution.py:188
  464.4 80.2 %reduce-scatter.45.cloned.1.call-start = ((), (), s32[]{:S(2)}) async-start(), calls=%async_computation.35 | async-start | bytes 163840 | tf_op jit(solution)/shard_map/reduce_scatter | solution.py:188
  473.9 93.5 %reduce-scatter.39.cloned.1.call-start = ((), (), s32[]{:S(2)}) async-start(), calls=%async_computation.32 | async-start | bytes 163840 | tf_op jit(solution)/shard_map/reduce_scatter | solution.py:188
  474.6 126.7 %reduce-scatter.49.cloned.1.call-start = ((), (), s32[]{:S(2)}) async-start(), calls=%async_computation.37 | async-start | bytes 2621440 | tf_op jit(solution)/shard_map/reduce_scatter | solution.py:188
  481.9 140.5 %reduce-scatter.33.cloned.1.call-start = ((), (), s32[]{:S(2)}) async-start(), calls=%async_computation.29 | async-start | bytes 491520 | tf_op jit(solution)/shard_map/reduce_scatter | solution.py:188
  493.5 152.0 %reduce-scatter.27.cloned.1.call-start = ((), (), s32[]{:S(2)}) async-start(), calls=%async_computation.26 | async-start | bytes 491520 | tf_op jit(solution)/shard_map/reduce_scatter | solution.py:188
  494.0 185.4 %reduce-scatter.67.cloned.1.call-start = ((), (), s32[]{:S(2)}) async-start(), calls=%async_computation.46 | async-start | bytes 2621440 | tf_op jit(solution)/shard_map/reduce_scatter | solution.py:188
  501.2 209.9 %reduce-scatter.61.cloned.1.call-start = ((), (), s32[]{:S(2)}) async-start(), calls=%async_computation.43 | async-start | bytes 2621440 | tf_op jit(solution)/shard_map/reduce_scatter | solution.py:188
  515.3 217.1 %reduce-scatter.57.cloned.1.call-start = ((), (), s32[]{:S(2)}) async-start(), calls=%async_computation.41 | async-start | bytes 655360 | tf_op jit(solution)/shard_map/reduce_scatter | solution.py:188
  524.2 230.9 %reduce-scatter.47.cloned.1.call-start = ((), (), s32[]{:S(2)}) async-start(), calls=%async_computation.36 | async-start | bytes 40960 | tf_op jit(solution)/shard_map/reduce_scatter | solution.py:188
  544.6 233.1 %reduce-scatter.41.cloned.1.call-start = ((), (), s32[]{:S(2)}) async-start(), calls=%async_computation.33 | async-start | bytes 40960 | tf_op jit(solution)/shard_map/reduce_scatter | solution.py:188
  567.4 233.7 %reduce-scatter.51.cloned.1.call-start = ((), (), s32[]{:S(2)}) async-start(), calls=%async_computation.38 | async-start | bytes 655360 | tf_op jit(solution)/shard_map/reduce_scatter | solution.py:188
  601.4 222.7 %reduce-scatter.35.cloned.1.call-start = ((), (), s32[]{:S(2)}) async-start(), calls=%async_computation.30 | async-start | bytes 122880 | tf_op jit(solution)/shard_map/reduce_scatter | solution.py:188
  622.4 224.4 %reduce-scatter.29.cloned.1.call-start = ((), (), s32[]{:S(2)}) async-start(), calls=%async_computation.27 | async-start | bytes 122880 | tf_op jit(solution)/shard_map/reduce_scatter | solution.py:188
  645.5 224.9 %reduce-scatter.69.cloned.1.call-start = ((), (), s32[]{:S(2)}) async-start(), calls=%async_computation.47 | async-start | bytes 655360 | tf_op jit(solution)/shard_map/reduce_scatter | solution.py:188
  679.4 214.7 %reduce-scatter.63.cloned.1.call-start = ((), (), s32[]{:S(2)}) async-start(), calls=%async_computation.44 | async-start | bytes 655360 | tf_op jit(solution)/shard_map/reduce_scatter | solution.py:188
  688.0 23.3 %collective-permute-start.12 = (bf16[4,1,192,512]{3,2,1,0:T(8,128)(2,1)S(1)}, bf16[4,1,192,512]{3,2,1,0:T(8,128)(2,1)}, u32[]{:S(2)}, u32[]{:S(2)}) collective-permute-start(bf16[4,1,192,512]{3,2,1,0:T(8,128)(2,1)S(1)} %constant_dynamic-slice_fusion), channel_id=1, source_target_pairs={{0,64},{64,0},{1,65},{65,1},{2,66},{66,2},{3,67},{67,3},{4,68},{68... | collective-permute-start | bytes 2359304 | tf_op jit(solution)/shard_map/ppermute | solution.py:175
  711.2 205.9 %reduce-scatter.59.cloned.1.call-start = ((), (), s32[]{:S(2)}) async-start(), calls=%async_computation.42 | async-start | bytes 163840 | tf_op jit(solution)/shard_map/reduce_scatter | solution.py:188
  732.4 207.3 %reduce-scatter.53.cloned.1.call-start = ((), (), s32[]{:S(2)}) async-start(), calls=%async_computation.39 | async-start | bytes 163840 | tf_op jit(solution)/shard_map/reduce_scatter | solution.py:188
  801.1 161.2 %reduce-scatter.71.cloned.1.call-start = ((), (), s32[]{:S(2)}) async-start(), calls=%async_computation.48 | async-start | bytes 163840 | tf_op jit(solution)/shard_map/reduce_scatter | solution.py:188
  847.6 23.5 %collective-permute-start.2 = (f32[8,768]{1,0:T(8,128)S(1)}, f32[8,768]{1,0:T(8,128)S(1)}, u32[]{:S(2)}, u32[]{:S(2)}) collective-permute-start(f32[8,768]{1,0:T(8,128)S(1)} %broadcast_select_fusion.12), channel_id=1, source_target_pairs={{0,64},{64,0},{1,65},{65,1},{2,66},{66,2},{3,67},{67,3},{4,68},{68... | collective-permute-start | bytes 73736 | tf_op jit(solution)/shard_map/ppermute | solution.py:194
  870.4 114.6 %reduce-scatter.65.cloned.1.call-start = ((), (), s32[]{:S(2)}) async-start(), calls=%async_computation.45 | async-start | bytes 163840 | tf_op jit(solution)/shard_map/reduce_scatter | solution.py:188
  940.5 48.3 %collective-permute-start.8 = (f32[8,1024]{1,0:T(8,128)S(1)}, f32[8,1024]{1,0:T(8,128)S(1)}, u32[]{:S(2)}, u32[]{:S(2)}) collective-permute-start(f32[8,1024]{1,0:T(8,128)S(1)} %broadcast_select_fusion.8), channel_id=1, source_target_pairs={{0,64},{64,0},{1,65},{65,1},{2,66},{66,2},{3,67},{67,3},{4,68},{68... | collective-permute-start | bytes 98312 | tf_op jit(solution)/shard_map/ppermute | solution.py:194
  (61 other events, 1011.3 us)
Sparse Core Ops, SparseCore 0:
  11.7 69.2 all-gather.7
  83.7 60.9 all-gather.11
  147.9 64.1 all-gather.13
  215.2 64.0 all-gather.9
  393.1 16.2 reduce-scatter.42
  411.6 21.4 reduce-scatter.36
  436.1 27.5 reduce-scatter.30
  466.1 25.5 reduce-scatter.24
  494.2 29.9 reduce-scatter.54
  526.3 18.2 reduce-scatter.44
  547.0 20.3 reduce-scatter.38
  569.7 31.6 reduce-scatter.48
  603.7 18.5 reduce-scatter.32
  624.6 20.7 reduce-scatter.26
  647.7 31.6 reduce-scatter.66
  681.6 29.4 reduce-scatter.60
  713.4 18.9 reduce-scatter.56
  734.6 20.4 reduce-scatter.46
  757.4 20.2 reduce-scatter.40
  779.9 21.1 reduce-scatter.50
  803.5 20.5 reduce-scatter.34
  826.5 20.3 reduce-scatter.28
  849.2 21.1 reduce-scatter.68
  872.6 21.4 reduce-scatter.62
  896.4 20.6 reduce-scatter.58
  919.3 20.3 reduce-scatter.52
  941.9 20.3 reduce-scatter.70
  964.7 20.3 reduce-scatter.64
